TPU v7x, 32 devices: a whole 2x2x4 slice. The times are simulated.
32 devices in a mesh: member: 2 (over x), lon: 8 (over z, y), lat: 2 (over core).
Axes of the slice: x: 2, y: 2, z: 4, core: 2. Of those that a mesh axis runs over, the one named last changes fastest.
Arguments:
- strain_rate: float32 [3, 256, 2160], P(None, 'lon', 'lat'), may hold values from -6 to 6
- stress_start: float32 [3, 256, 2160], P(None, 'lon', 'lat'), may hold values from -3 to 3
- concentration: float32 [256, 2160], P('lon', 'lat'), may hold values from 0.5 to 1
- cell_class: int32 [512, 2160], P(('member', 'lon'), 'lat'), parts along dimension 0, may hold values from 0 to 7
- land_mask: int32 [256, 2160], P('lon', 'lat'), may hold values 0 or 1
- fold_partner: int32 [256], replicated, may hold values from 0 to 255, each once
- kernel_weights: float32 [7, 7], replicated, may hold values from 0.05 to 0.5
Outputs:
- stress_out: float32 [3, 512, 2160], P(None, ('member', 'lon'), 'lat'), parts along dimension 1
- damage_out: float32 [512, 2160], P(('member', 'lon'), 'lat'), parts along dimension 0
- mean_overstress: float32 [6], P('member'), parts along dimension 0
There are 2 independent parts, one for each index of `member`. A program takes and returns all parts, laid end to end along the dimension named above; an argument that names none is the same for every part. Nothing has to cross between parts.
Inputs may be any that keep to these rules, and one draw needn't show every extreme that they name: `fold_partner`: each of the 256 longitude indices appears once.
All inputs are finite; a program needn't handle non-finite values. No bound on the sum of `land_mask` on one device may be relied on, other than what follows from the above.
Results may differ from a plain program's by a relative error of at most 0.0001.
Values sent between devices are 32-bit elements; how exact they have to be, the bound alone decides.
A program may use at most 64 MiB of HBM per device.

v0:
```python
import jax
import jax.numpy as jnp
from jax import lax
from jax.sharding import PartitionSpec as P

ITERS = 3


def padded_2(array, sides, width):
    for axis, dim in sides:
        size, length = (lax.axis_size(axis), array.shape[dim])
        up = [(i, (i + 1) % size) for i in range(size)]
        down = [(j, i) for i, j in up]
        last = lax.slice_in_dim(array, length - width, length, axis=dim)
        first = lax.slice_in_dim(array, 0, width, axis=dim)
        before = lax.ppermute(last, axis, up)
        after = lax.ppermute(first, axis, down)
        array = jnp.concatenate([before, array, after], axis=dim)
    return array


def smooth(padded, weights, ncols, nrows):
    side = weights.shape[0]
    total = jnp.zeros((padded.shape[0], ncols, nrows), jnp.float32)
    for first in range(side):
        for second in range(side):
            total = (
                total
                + weights[first, second] * padded[:, first : first + ncols, second : second + nrows]
            )
    return total


def extend(fields, partner, width):
    ncols = fields.shape[1]
    top = jnp.swapaxes(fields[:, :, -width:], 1, 2)
    whole_top = lax.all_gather(top, "lon", axis=2, tiled=True)
    total_cols = whole_top.shape[2]
    first_col = lax.axis_index("lon") * ncols
    columns = (first_col - width + jnp.arange(ncols + 2 * width, dtype=jnp.int32)) % total_cols
    picked = jnp.take(partner, columns)
    rows = jnp.take(whole_top, picked, axis=2)
    north = jnp.swapaxes(rows[:, ::-1, :], 1, 2)
    lat_place = lax.axis_index("lat")
    lat_last = lax.axis_size("lat") - 1
    padded = padded_2(fields, (("lon", 1), ("lat", 2)), width)
    south_rim = jnp.where(
        lat_place == 0, jnp.zeros_like(padded[:, :, :width]), padded[:, :, :width]
    )
    north_rim = jnp.where(lat_place == lat_last, north, padded[:, :, -width:])
    return jnp.concatenate([south_rim, padded[:, :, width:-width], north_rim], axis=2)


def ocean_excess(local_excess, count):
    excess, ocean_total = lax.psum((local_excess, count), ("lon", "lat"))
    return excess / (ocean_total + 1.0)


def shards(
    strain_rate, stress_start, concentration, cell_class, land_mask, fold_partner, kernel_weights
):
    width = kernel_weights.shape[0] // 2
    ocean = land_mask.astype(jnp.float32)
    ncols, nrows = ocean.shape
    denom = smooth(extend(ocean[None], fold_partner, width), kernel_weights, ncols, nrows)[0] + 1.0
    count = jnp.sum(ocean)
    damage = ocean * 0.1 * cell_class.astype(jnp.float32) * concentration
    stress = ocean[None] * stress_start
    base = concentration * jnp.exp(-2.0 * (1.0 - concentration))
    e_one, e_two, e_shear = (strain_rate[0], strain_rate[1], strain_rate[2])
    load = jnp.stack([e_one + e_two / 3.0, e_two + e_one / 3.0, e_shear / (4.0 / 3.0)]) / (
        8.0 / 9.0
    )
    means = []
    for step in range(ITERS):
        keep = 1.0 - damage
        theta = 0.5 / (keep * keep)
        elastic = ocean[None] * (stress + (base * keep)[None] * load) / (1.0 + theta)[None]
        half_diff = (elastic[0] - elastic[1]) / 2.0
        tau = jnp.sqrt(half_diff * half_diff + elastic[2] * elastic[2] + 0.25)
        ratio = (tau + 0.7 * (elastic[0] + elastic[1]) / 2.0) / (0.6 * concentration)
        over = jnp.maximum(ratio, 1.0)
        q_part = 1.0 - 1.0 / over
        local_excess = jnp.sum(ocean * (over - 1.0))
        mean_now = ocean_excess(local_excess, count)
        factor = 1.0 / (1.0 + 2.0 * mean_now)
        local_damage = ocean * (damage + factor * keep * q_part)
        local_stress = elastic * (1.0 - factor * q_part)[None]
        fields = jnp.concatenate([local_damage[None], local_stress], axis=0)
        averaged = (
            smooth(extend(fields, fold_partner, width), kernel_weights, ncols, nrows) / denom[None]
        )
        fresh = ocean[None] * (0.5 * fields + 0.5 * averaged)
        means.append(mean_now)
        damage = fresh[0]
        stress = fresh[1:]
    return (stress, damage, jnp.stack(means))


def solution(mesh):
    in_specs = (
        P(None, "lon", "lat"),
        P(None, "lon", "lat"),
        P("lon", "lat"),
        P(("member", "lon"), "lat"),
        P("lon", "lat"),
        P(),
        P(),
    )
    out_specs = (P(None, ("member", "lon"), "lat"), P(("member", "lon"), "lat"), P("member"))
    return jax.shard_map(shards, mesh=mesh, in_specs=in_specs, out_specs=out_specs, check_vma=False)
```

profile of v0, /device:TPU:0, one launch (start us, length us, event | category | flops | bytes accessed | tf_op | source)
XLA Modules:
  0.0 402.8 jit_solution(4473305265631229765)
XLA Ops:
  0.7 1.0 convert_bitcast_fusion
  1.7 3.0 collective-permute-start.4
  4.7 3.1 collective-permute-start.5
  7.9 0.1 multiply_multiply_fusion.2
  8.0 0.9 copy-done.3
  8.9 0.1 multiply_divide_fusion
  9.0 0.7 convert_reduce_fusion
  9.8 30.9 %all-reduce = (f32[]{:T(128)}, f32[]{:T(128)}) all-reduce(f32[]{:T(128)} %get-tuple-element.12, f32[]{:T(128)} %get-tuple-element.11), channel_id=1, replica_groups=mesh['member'=2,'lon'=8,'lat'=2] {'lon','lat'}, use_global_device_ids=true, to_apply=%region_1.2 | all-reduce | flops 2 | bytes 16 | tf_op jit(solution)/shard_map/psum | solution.py:55
  42.1 0.1 broadcast_multiply_fusion.2
  42.3 4.7 %collective-permute-start.1 = (f32[4,3,1080]{2,1,0:T(4,128)S(1)}, f32[4,3,1080]{2,1,0:T(4,128)S(1)}, u32[]{:S(2)}, u32[]{:S(2)}) collective-permute-start(f32[4,3,1080]{2,1,0:T(4,128)S(1)} %get-tuple-element.45), channel_id=1, source_target_pairs={{2,0},{4,2},{6,4},{8,6},{10,8},{12,10},{14,12},{0,14},{3,1},{5,3},... | collective-permute-start | bytes 155528 | tf_op jit(solution)/shard_map/ppermute | solution.py:17
  47.0 0.7 fusion.262
  47.8 0.7 fusion.263
  48.7 0.8 gather_fusion.1
  49.5 30.5 %all_gather.13 = f32[1,3,256]{1,2,0:T(8,128)S(1)} all-gather(f32[1,3,32]{1,2,0:T(8,128)S(1)} %slice_bitcast_fusion.1), channel_id=1, replica_groups=mesh['member'=2,'lon'=8,'lat'=2] {'lon'}, dimensions={2}, use_global_device_ids=true | all-gather | bytes 3456 | tf_op jit(solution)/shard_map/all_gather | solution.py:37
  80.1 31.2 %all_gather.12 = f32[4,3,256]{1,0,2:T(4,128)S(1)} all-gather(f32[4,3,32]{1,0,2:T(4,128)S(1)} %copy.60), channel_id=1, replica_groups=mesh['member'=2,'lon'=8,'lat'=2] {'lon'}, dimensions={2}, use_global_device_ids=true | all-gather | bytes 13824 | tf_op jit(solution)/shard_map/all_gather | solution.py:37
  111.3 0.6 gather_fusion
  111.8 0.6 gather_fusion.2
  112.6 0.7 fusion.264
  113.5 0.1 rev.12
  113.6 0.6 collective-permute-start.7
  114.1 0.5 collective-permute-done.6
  114.6 0.4 collective-permute-done.7
  115.0 0.1 maximum_maximum_fusion.6
  115.1 31.9 %fusion.171 = f32[32,1080]{1,0:T(8,128)S(1)} fusion(f32[1,32,1080]{2,1,0:T(8,128)S(1)} %get-tuple-element.61, f32[1,3,1080]{2,1,0:T(4,128)S(1)} %collective-permute-done.5, f32[1,3,1080]{2,1,0:T(4,128)S(1)} %collective-permute-done.4, f32[1,38,1083]{2,1,0:T(8,128)S(1)} %get-tuple-element.52, f32[1,38,1083]{2,1,0:T(8,128)S(1)} %get-tuple-element.51, ...), kind=kLoop, calls=%fused_computation.370 | loop fusion | flops 3628800 | bytes 6246916 | tf_op jit(solution)/shard_map/div | solution.py:91
  147.1 0.1 pad_maximum_fusion.24
  147.2 0.4 collective-permute-start.2
  147.6 0.2 collective-permute-start.3
  147.7 0.1 maximum_maximum_fusion.1
  147.8 0.7 collective-permute-done.2
  148.5 0.3 collective-permute-done.3
  148.9 0.4 maximum_maximum_fusion
  149.2 36.4 %fusion.105 = f32[4,32,1080]{2,1,0:T(8,128)S(1)} fusion(f32[4,38,1083]{2,1,0:T(8,128)S(1)} %get-tuple-element.31, f32[4,35,1080]{2,1,0:T(8,128)S(1)} %get-tuple-element.43, f32[4,38,1083]{2,1,0:T(8,128)S(1)} %get-tuple-element.30, f32[4,35,1080]{2,1,0:T(8,128)S(1)} %get-tuple-element.42, f32[3,32,1080]{2,1,0:T(8,128)S(1)} %broadcast_multiply_fusion.2, ...), kind=kLoop, calls=%fused_computation.240 | loop fusion | flops 13962240 | bytes 27924676 | tf_op jit(solution)/shard_map/mul | solution.py:93
  185.8 0.7 multiply_reduce_fusion.1
  186.5 30.3 %psum.36 = f32[]{:T(128)} all-reduce(f32[]{:T(128)} %get-tuple-element.17), channel_id=1, replica_groups=mesh['member'=2,'lon'=8,'lat'=2] {'lon','lat'}, use_global_device_ids=true, to_apply=%region_5.8 | all-reduce | flops 1 | bytes 8 | tf_op jit(solution)/shard_map/psum | solution.py:55
  217.6 0.1 broadcast_multiply_fusion.1
  217.7 0.1 fusion.254
  217.9 4.7 %collective-permute-start.9 = (f32[4,3,1080]{2,1,0:T(4,128)S(1)}, f32[4,3,1080]{2,1,0:T(4,128)S(1)}, u32[]{:S(2)}, u32[]{:S(2)}) collective-permute-start(f32[4,3,1080]{2,1,0:T(4,128)S(1)} %get-tuple-element.41), channel_id=1, source_target_pairs={{2,0},{4,2},{6,4},{8,6},{10,8},{12,10},{14,12},{0,14},{3,1},{5,3},... | collective-permute-start | bytes 155528 | tf_op jit(solution)/shard_map/ppermute | solution.py:17
  222.6 31.4 %all_gather.14 = f32[4,3,256]{1,0,2:T(4,128)S(1)} all-gather(f32[4,3,32]{1,0,2:T(4,128)S(1)} %copy.64), channel_id=1, replica_groups=mesh['member'=2,'lon'=8,'lat'=2] {'lon'}, dimensions={2}, use_global_device_ids=true | all-gather | bytes 13824 | tf_op jit(solution)/shard_map/all_gather | solution.py:37
  254.0 0.6 gather_fusion.3
  254.7 0.1 rev.14
  254.8 0.1 pad_maximum_fusion.20
  255.0 0.5 collective-permute-start.11
  255.5 0.1 maximum_maximum_fusion.3
  255.6 0.7 collective-permute-done.10
  256.3 0.1 collective-permute-done.11
  256.4 0.4 maximum_maximum_fusion.2
  256.8 36.4 %fusion.54 = f32[4,32,1080]{2,1,0:T(8,128)S(1)} fusion(f32[4,38,1083]{2,1,0:T(8,128)S(1)} %get-tuple-element.27, f32[4,35,1080]{2,1,0:T(8,128)S(1)} %get-tuple-element.39, f32[4,38,1083]{2,1,0:T(8,128)S(1)} %get-tuple-element.26, f32[4,35,1080]{2,1,0:T(8,128)S(1)} %get-tuple-element.38, f32[3,32,1080]{2,1,0:T(8,128)S(1)} %broadcast_multiply_fusion.1, ...), kind=kLoop, calls=%fused_computation.141 | loop fusion | flops 13962240 | bytes 27924676 | tf_op jit(solution)/shard_map/mul | solution.py:93
  293.3 0.7 multiply_reduce_fusion
  294.1 30.4 %psum.37 = f32[]{:T(128)} all-reduce(f32[]{:T(128)} %get-tuple-element.15), channel_id=1, replica_groups=mesh['member'=2,'lon'=8,'lat'=2] {'lon','lat'}, use_global_device_ids=true, to_apply=%region_7.10 | all-reduce | flops 1 | bytes 8 | tf_op jit(solution)/shard_map/psum | solution.py:55
  325.3 0.1 broadcast_multiply_fusion
  325.4 0.1 fusion.252
  325.6 4.7 %collective-permute-start.13 = (f32[4,3,1080]{2,1,0:T(4,128)S(1)}, f32[4,3,1080]{2,1,0:T(4,128)S(1)}, u32[]{:S(2)}, u32[]{:S(2)}) collective-permute-start(f32[4,3,1080]{2,1,0:T(4,128)S(1)} %get-tuple-element.37), channel_id=1, source_target_pairs={{2,0},{4,2},{6,4},{8,6},{10,8},{12,10},{14,12},{0,14},{3,1},{5,3},... | collective-permute-start | bytes 155528 | tf_op jit(solution)/shard_map/ppermute | solution.py:17
  330.3 31.2 %all_gather.15 = f32[4,3,256]{1,0,2:T(4,128)S(1)} all-gather(f32[4,3,32]{1,0,2:T(4,128)S(1)} %copy.66), channel_id=1, replica_groups=mesh['member'=2,'lon'=8,'lat'=2] {'lon'}, dimensions={2}, use_global_device_ids=true | all-gather | bytes 13824 | tf_op jit(solution)/shard_map/all_gather | solution.py:37
  361.5 0.6 gather_fusion.4
  362.2 0.6 pad_maximum_fusion.28
  362.9 0.1 pad_maximum_fusion.16
  363.1 0.5 collective-permute-start.15
  363.6 0.1 maximum_maximum_fusion.5
  363.7 0.7 collective-permute-done.14
  364.4 0.1 collective-permute-done.15
  364.5 0.4 maximum_maximum_fusion.4
  364.9 36.4 %fusion.3 = f32[4,32,1080]{2,1,0:T(8,128)S(1)} fusion(f32[4,38,1083]{2,1,0:T(8,128)S(1)} %get-tuple-element.23, f32[4,35,1080]{2,1,0:T(8,128)S(1)} %get-tuple-element.35, f32[4,38,1083]{2,1,0:T(8,128)S(1)} %get-tuple-element.22, f32[4,35,1080]{2,1,0:T(8,128)S(1)} %get-tuple-element.34, f32[3,32,1080]{2,1,0:T(8,128)S(1)} %broadcast_multiply_fusion, ...), kind=kLoop, calls=%fused_computation.42 | loop fusion | flops 13962240 | bytes 27924676 | tf_op jit(solution)/shard_map/mul | solution.py:93
  401.3 0.7 slice_bitcast_fusion
  402.0 0.8 slice.1702
  (65 shorter events, 1.9 us)
Async XLA Ops:
  0.6 48.1 %copy-start = (s32[256]{0:T(256)S(1)}, s32[256]{0:T(256)}, u32[]{:S(2)}) copy-start(s32[256]{0:T(256)} %param.16) | copy-start | bytes 3076
  0.6 7.2 %copy-start.5 = (f32[3,32,1080]{2,1,0:T(8,128)S(1)}, f32[3,32,1080]{2,1,0:T(8,128)}, u32[]{:S(2)}) copy-start(f32[3,32,1080]{2,1,0:T(8,128)} %param.11) | copy-start | bytes 1244164
  1.7 111.6 %collective-permute-start.4 = (f32[1,3,1080]{2,1,0:T(4,128)S(1)}, f32[1,3,1080]{2,1,0:T(4,128)S(1)}, u32[]{:S(2)}, u32[]{:S(2)}) collective-permute-start(f32[1,3,1080]{2,1,0:T(4,128)S(1)} %get-tuple-element.59), channel_id=1, source_target_pairs={{0,2},{2,4},{4,6},{6,8},{8,10},{10,12},{12,14},{14,0},{1,3},{3,5},... | collective-permute-start | bytes 38888 | tf_op jit(solution)/shard_map/ppermute | solution.py:16
  4.7 3.2 copy-start.1
  4.7 3.2 copy-start.2
  4.7 3.2 copy-start.4
  4.7 108.6 %collective-permute-start.5 = (f32[1,3,1080]{2,1,0:T(4,128)S(1)}, f32[1,3,1080]{2,1,0:T(4,128)S(1)}, u32[]{:S(2)}, u32[]{:S(2)}) collective-permute-start(f32[1,3,1080]{2,1,0:T(4,128)S(1)} %get-tuple-element.60), channel_id=1, source_target_pairs={{2,0},{4,2},{6,4},{8,6},{10,8},{12,10},{14,12},{0,14},{3,1},{5,3},... | collective-permute-start | bytes 38888 | tf_op jit(solution)/shard_map/ppermute | solution.py:17
  7.9 1.0 copy-start.3
  42.3 4.8 %copy-start.6 = (f32[7,7]{1,0:T(8,128)S(1)}, f32[7,7]{1,0:T(8,128)}, u32[]{:S(2)}) copy-start(f32[7,7]{1,0:T(8,128)} %param.17) | copy-start | bytes 592
  42.3 104.8 %collective-permute-start = (f32[4,3,1080]{2,1,0:T(4,128)S(1)}, f32[4,3,1080]{2,1,0:T(4,128)S(1)}, u32[]{:S(2)}, u32[]{:S(2)}) collective-permute-start(f32[4,3,1080]{2,1,0:T(4,128)S(1)} %get-tuple-element.44), channel_id=1, source_target_pairs={{0,2},{2,4},{4,6},{6,8},{8,10},{10,12},{12,14},{14,0},{1,3},{3,5},... | collective-permute-start | bytes 155528 | tf_op jit(solution)/shard_map/ppermute | solution.py:16
  42.3 104.7 %collective-permute-start.1 = (f32[4,3,1080]{2,1,0:T(4,128)S(1)}, f32[4,3,1080]{2,1,0:T(4,128)S(1)}, u32[]{:S(2)}, u32[]{:S(2)}) collective-permute-start(f32[4,3,1080]{2,1,0:T(4,128)S(1)} %get-tuple-element.45), channel_id=1, source_target_pairs={{2,0},{4,2},{6,4},{8,6},{10,8},{12,10},{14,12},{0,14},{3,1},{5,3},... | collective-permute-start | bytes 155528 | tf_op jit(solution)/shard_map/ppermute | solution.py:17
  113.4 1.2 collective-permute-start.6
  113.6 1.4 collective-permute-start.7
  147.2 1.3 collective-permute-start.2
  147.6 1.3 collective-permute-start.3
  217.8 36.9 %collective-permute-start.8 = (f32[4,3,1080]{2,1,0:T(4,128)S(1)}, f32[4,3,1080]{2,1,0:T(4,128)S(1)}, u32[]{:S(2)}, u32[]{:S(2)}) collective-permute-start(f32[4,3,1080]{2,1,0:T(4,128)S(1)} %get-tuple-element.40), channel_id=1, source_target_pairs={{0,2},{2,4},{4,6},{6,8},{8,10},{10,12},{12,14},{14,0},{1,3},{3,5},... | collective-permute-start | bytes 155528 | tf_op jit(solution)/shard_map/ppermute | solution.py:16
  217.9 36.9 %collective-permute-start.9 = (f32[4,3,1080]{2,1,0:T(4,128)S(1)}, f32[4,3,1080]{2,1,0:T(4,128)S(1)}, u32[]{:S(2)}, u32[]{:S(2)}) collective-permute-start(f32[4,3,1080]{2,1,0:T(4,128)S(1)} %get-tuple-element.41), channel_id=1, source_target_pairs={{2,0},{4,2},{6,4},{8,6},{10,8},{12,10},{14,12},{0,14},{3,1},{5,3},... | collective-permute-start | bytes 155528 | tf_op jit(solution)/shard_map/ppermute | solution.py:17
  254.9 1.3 collective-permute-start.10
  255.0 1.4 collective-permute-start.11
  325.6 37.3 %collective-permute-start.12 = (f32[4,3,1080]{2,1,0:T(4,128)S(1)}, f32[4,3,1080]{2,1,0:T(4,128)S(1)}, u32[]{:S(2)}, u32[]{:S(2)}) collective-permute-start(f32[4,3,1080]{2,1,0:T(4,128)S(1)} %get-tuple-element.36), channel_id=1, source_target_pairs={{0,2},{2,4},{4,6},{6,8},{8,10},{10,12},{12,14},{14,0},{1,3},{3,5},... | collective-permute-start | bytes 155528 | tf_op jit(solution)/shard_map/ppermute | solution.py:16
  325.6 37.3 %collective-permute-start.13 = (f32[4,3,1080]{2,1,0:T(4,128)S(1)}, f32[4,3,1080]{2,1,0:T(4,128)S(1)}, u32[]{:S(2)}, u32[]{:S(2)}) collective-permute-start(f32[4,3,1080]{2,1,0:T(4,128)S(1)} %get-tuple-element.37), channel_id=1, source_target_pairs={{2,0},{4,2},{6,4},{8,6},{10,8},{12,10},{14,12},{0,14},{3,1},{5,3},... | collective-permute-start | bytes 155528 | tf_op jit(solution)/shard_map/ppermute | solution.py:17
  363.0 1.3 collective-permute-start.14
  363.1 1.4 collective-permute-start.15
where the time goes:
time: 405 us; the launch traced here: 403 us
  blocking collectives  216 us (53%)
  other arithmetic  148 us (37%)
  starting transfers between devices  22.8 us (6%)
  local copies, waits for them, and re-layouts  8.27 us (2%)
    all_gather x4, blocking collectives, extend(): whole_top = lax.all_gather(top, 'lon', axis=2, tiled=True)  124 us
    mul x3, other arithmetic, shards(): fresh = ocean[None] * (0.5 * fields + 0.5 * averaged)  109 us
    psum x3, blocking collectives, ocean_excess(): excess, ocean_total = lax.psum((local_excess, count), ('lon', 'lat'))  91.6 us
    div x1, other arithmetic, shards(): smooth(extend(fields, fold_partner, width), kernel_weights, ncols, nrows)  31.9 us
    ppermute x8, starting transfers between devices, padded_2(): after = lax.ppermute(first, axis, down)  19 us
  transfers between devices with their start and end apart: 16, of which 8 were waited for; matrix products, arithmetic and copies ran while one was open for 10% of the time, Pallas kernels for 0%

commit v1 on v0

--- a/solution.py
+++ b/solution.py
@@ -34,7 +34,12 @@
 def extend(fields, partner, width):
     ncols = fields.shape[1]
     top = jnp.swapaxes(fields[:, :, -width:], 1, 2)
-    whole_top = lax.all_gather(top, "lon", axis=2, tiled=True)
+    ring = [top]
+    for hop in range(7):
+        ring.append(lax.ppermute(ring[-1], "lon", [(dev, (dev + 1) % 8) for dev in range(8)]))
+    whole_top = jnp.roll(
+        jnp.concatenate(ring[::-1], axis=2), (lax.axis_index("lon") + 1) * ring[0].shape[2], axis=2
+    )
     total_cols = whole_top.shape[2]
     first_col = lax.axis_index("lon") * ncols
     columns = (first_col - width + jnp.arange(ncols + 2 * width, dtype=jnp.int32)) % total_cols

time: 405 us -> 435 us (1.074)
  waiting for transfers between devices: 3.48 us -> 152 us
  blocking collectives: 216 us -> 94.2 us
    ppermute x0 -> x28, waiting for transfers between devices: none -> 148 us  [extend(): lax.ppermute(ring[-1], 'lon', [(dev, (dev + 1) % 8) for dev in range(8)])]
    all_gather x4 -> x0, blocking collectives: 124 us -> none  [extend(): whole_top = lax.all_gather(top, 'lon', axis=2, tiled=True)]
    ppermute x0 -> x28, starting transfers between devices: none -> 5.27 us  [extend(): lax.ppermute(ring[-1], 'lon', [(dev, (dev + 1) % 8) for dev in range(8)])]
  transfers between devices with their start and end apart: 16 -> 44, of which waited for: 8 -> 33; matrix products, arithmetic and copies ran while one was open for 10% -> 10% of each run, Pallas kernels for 0% -> 0%
where the time goes in v1:
time: 435 us; the launch traced here: 433 us
  waiting for transfers between devices  152 us (35%)
  other arithmetic  149 us (34%)
  blocking collectives  94.2 us (22%)
  starting transfers between devices  22.2 us (5%)
  local copies, waits for them, and re-layouts  12.5 us (3%)
    ppermute x28, waiting for transfers between devices, extend(): lax.ppermute(ring[-1], 'lon', [(dev, (dev + 1) % 8) for dev in range(8)])  148 us
    mul x3, other arithmetic, shards(): fresh = ocean[None] * (0.5 * fields + 0.5 * averaged)  109 us
    psum x3, blocking collectives, ocean_excess(): excess, ocean_total = lax.psum((local_excess, count), ('lon', 'lat'))  94.2 us
    div x1, other arithmetic, shards(): smooth(extend(fields, fold_partner, width), kernel_weights, ncols, nrows)  32 us
    ppermute x8, starting transfers between devices, padded_2(): after = lax.ppermute(first, axis, down)  14.6 us
  transfers between devices with their start and end apart: 44, of which 33 were waited for; matrix products, arithmetic and copies ran while one was open for 10% of the time, Pallas kernels for 0%

profile of v1, /device:TPU:0, one launch (start us, length us, event | category | flops | bytes accessed | tf_op | source)
XLA Modules:
  0.0 433.4 jit_solution(11765827114871954379)
XLA Ops:
  0.7 1.0 convert_bitcast_fusion
  1.7 3.0 collective-permute-start.14
  4.7 1.6 collective-permute-start.11
  6.3 3.2 collective-permute-start.12
  9.7 0.9 copy-done.3
  10.7 0.7 convert_reduce_fusion
  11.4 30.1 %all-reduce = (f32[]{:T(128)}, f32[]{:T(128)}) all-reduce(f32[]{:T(128)} %get-tuple-element.16, f32[]{:T(128)} %get-tuple-element.15), channel_id=1, replica_groups=mesh['member'=2,'lon'=8,'lat'=2] {'lon','lat'}, use_global_device_ids=true, to_apply=%region_1.2 | all-reduce | flops 2 | bytes 16 | tf_op jit(solution)/shard_map/psum | solution.py:60
  43.4 0.8 gather_fusion.1
  44.2 0.7 fusion.265
  44.9 5.6 %collective-permute-done.3 = f32[4,3,32]{1,2,0:T(8,128)S(1)} collective-permute-done((f32[4,3,32]{1,2,0:T(8,128)S(1)}, f32[4,3,32]{1,2,0:T(8,128)S(1)}, u32[]{:S(2)}, u32[]{:S(2)}) %collective-permute-start.3) | collective-permute-done | bytes 1568 | tf_op jit(solution)/shard_map/ppermute | solution.py:39
  50.5 0.7 fusion.266
  51.3 6.2 %collective-permute-done.4 = f32[4,3,32]{1,2,0:T(8,128)S(1)} collective-permute-done((f32[4,3,32]{1,2,0:T(8,128)S(1)}, f32[4,3,32]{1,2,0:T(8,128)S(1)}, u32[]{:S(2)}, u32[]{:S(2)}) %collective-permute-start.4) | collective-permute-done | bytes 1568 | tf_op jit(solution)/shard_map/ppermute | solution.py:39
  57.5 0.7 fusion.267
  58.3 6.2 %collective-permute-done.5 = f32[4,3,32]{1,2,0:T(8,128)S(1)} collective-permute-done((f32[4,3,32]{1,2,0:T(8,128)S(1)}, f32[4,3,32]{1,2,0:T(8,128)S(1)}, u32[]{:S(2)}, u32[]{:S(2)}) %collective-permute-start.5) | collective-permute-done | bytes 1568 | tf_op jit(solution)/shard_map/ppermute | solution.py:39
  64.7 6.9 %collective-permute-done.16 = f32[1,3,32]{1,2,0:T(8,128)S(1)} collective-permute-done((f32[1,3,32]{1,2,0:T(8,128)S(1)}, f32[1,3,32]{1,2,0:T(8,128)S(1)}, u32[]{:S(2)}, u32[]{:S(2)}) %collective-permute-start.16) | collective-permute-done | bytes 416 | tf_op jit(solution)/shard_map/ppermute | solution.py:39
  71.6 6.4 %collective-permute-done.17 = f32[1,3,32]{1,2,0:T(8,128)S(1)} collective-permute-done((f32[1,3,32]{1,2,0:T(8,128)S(1)}, f32[1,3,32]{1,2,0:T(8,128)S(1)}, u32[]{:S(2)}, u32[]{:S(2)}) %collective-permute-start.17) | collective-permute-done | bytes 416 | tf_op jit(solution)/shard_map/ppermute | solution.py:39
  78.2 6.3 %collective-permute-done.18 = f32[1,3,32]{1,2,0:T(8,128)S(1)} collective-permute-done((f32[1,3,32]{1,2,0:T(8,128)S(1)}, f32[1,3,32]{1,2,0:T(8,128)S(1)}, u32[]{:S(2)}, u32[]{:S(2)}) %collective-permute-start.18) | collective-permute-done | bytes 416 | tf_op jit(solution)/shard_map/ppermute | solution.py:39
  84.5 6.5 %collective-permute-done.19 = f32[1,3,32]{1,2,0:T(8,128)S(1)} collective-permute-done((f32[1,3,32]{1,2,0:T(8,128)S(1)}, f32[1,3,32]{1,2,0:T(8,128)S(1)}, u32[]{:S(2)}, u32[]{:S(2)}) %collective-permute-start.19) | collective-permute-done | bytes 416 | tf_op jit(solution)/shard_map/ppermute | solution.py:39
  91.6 5.9 %collective-permute-done.20 = f32[1,3,32]{1,2,0:T(8,128)S(1)} collective-permute-done((f32[1,3,32]{1,2,0:T(8,128)S(1)}, f32[1,3,32]{1,2,0:T(8,128)S(1)}, u32[]{:S(2)}, u32[]{:S(2)}) %collective-permute-start.20) | collective-permute-done | bytes 416 | tf_op jit(solution)/shard_map/ppermute | solution.py:39
  97.7 2.1 collective-permute-start.8
  100.0 0.6 gather_fusion
  100.6 4.1 collective-permute-done.8
  105.3 6.3 %collective-permute-done.9 = f32[4,3,32]{1,2,0:T(8,128)S(1)} collective-permute-done((f32[4,3,32]{1,2,0:T(8,128)S(1)}, f32[4,3,32]{1,2,0:T(8,128)S(1)}, u32[]{:S(2)}, u32[]{:S(2)}) %collective-permute-start.9) | collective-permute-done | bytes 1568 | tf_op jit(solution)/shard_map/ppermute | solution.py:39
  112.2 0.6 gather_fusion.2
  113.1 0.6 collective-permute-start.21
  113.7 0.5 collective-permute-done.13
  114.2 0.4 collective-permute-done.21
  114.7 32.0 %fusion.171 = f32[32,1080]{1,0:T(8,128)S(1)} fusion(f32[1,32,1080]{2,1,0:T(8,128)S(1)} %get-tuple-element.65, f32[1,3,1080]{2,1,0:T(4,128)S(1)} %collective-permute-done.12, f32[1,3,1080]{2,1,0:T(4,128)S(1)} %collective-permute-done.11, f32[1,38,1083]{2,1,0:T(8,128)S(1)} %get-tuple-element.56, f32[1,38,1083]{2,1,0:T(8,128)S(1)} %get-tuple-element.55, ...), kind=kLoop, calls=%fused_computation.370 | loop fusion | flops 3628800 | bytes 6246916 | tf_op jit(solution)/shard_map/div | solution.py:96
  146.8 0.4 collective-permute-start.2
  147.5 0.7 collective-permute-done.2
  148.5 0.4 maximum_maximum_fusion
  148.9 36.4 %fusion.105 = f32[4,32,1080]{2,1,0:T(8,128)S(1)} fusion(f32[4,38,1083]{2,1,0:T(8,128)S(1)} %get-tuple-element.35, f32[4,35,1080]{2,1,0:T(8,128)S(1)} %get-tuple-element.47, f32[4,38,1083]{2,1,0:T(8,128)S(1)} %get-tuple-element.34, f32[4,35,1080]{2,1,0:T(8,128)S(1)} %get-tuple-element.46, f32[3,32,1080]{2,1,0:T(8,128)S(1)} %broadcast_multiply_fusion.2, ...), kind=kLoop, calls=%fused_computation.240 | loop fusion | flops 13962240 | bytes 27924676 | tf_op jit(solution)/shard_map/mul | solution.py:98
  185.5 0.7 multiply_reduce_fusion.1
  186.2 30.3 %psum.36 = f32[]{:T(128)} all-reduce(f32[]{:T(128)} %get-tuple-element.21), channel_id=1, replica_groups=mesh['member'=2,'lon'=8,'lat'=2] {'lon','lat'}, use_global_device_ids=true, to_apply=%region_5.9 | all-reduce | flops 1 | bytes 8 | tf_op jit(solution)/shard_map/psum | solution.py:60
  217.4 6.9 %collective-permute-done.25 = f32[4,3,32]{1,2,0:T(8,128)S(1)} collective-permute-done((f32[4,3,32]{1,2,0:T(8,128)S(1)}, f32[4,3,32]{1,2,0:T(8,128)S(1)}, u32[]{:S(2)}, u32[]{:S(2)}) %collective-permute-start.25) | collective-permute-done | bytes 1568 | tf_op jit(solution)/shard_map/ppermute | solution.py:39
  224.4 7.0 %collective-permute-done.26 = f32[4,3,32]{1,2,0:T(8,128)S(1)} collective-permute-done((f32[4,3,32]{1,2,0:T(8,128)S(1)}, f32[4,3,32]{1,2,0:T(8,128)S(1)}, u32[]{:S(2)}, u32[]{:S(2)}) %collective-permute-start.26) | collective-permute-done | bytes 1568 | tf_op jit(solution)/shard_map/ppermute | solution.py:39
  231.3 7.0 %collective-permute-done.27 = f32[4,3,32]{1,2,0:T(8,128)S(1)} collective-permute-done((f32[4,3,32]{1,2,0:T(8,128)S(1)}, f32[4,3,32]{1,2,0:T(8,128)S(1)}, u32[]{:S(2)}, u32[]{:S(2)}) %collective-permute-start.27) | collective-permute-done | bytes 1568 | tf_op jit(solution)/shard_map/ppermute | solution.py:39
  238.3 7.0 %collective-permute-done.28 = f32[4,3,32]{1,2,0:T(8,128)S(1)} collective-permute-done((f32[4,3,32]{1,2,0:T(8,128)S(1)}, f32[4,3,32]{1,2,0:T(8,128)S(1)}, u32[]{:S(2)}, u32[]{:S(2)}) %collective-permute-start.28) | collective-permute-done | bytes 1568 | tf_op jit(solution)/shard_map/ppermute | solution.py:39
  245.3 7.6 %collective-permute-done.29 = f32[4,3,32]{1,2,0:T(8,128)S(1)} collective-permute-done((f32[4,3,32]{1,2,0:T(8,128)S(1)}, f32[4,3,32]{1,2,0:T(8,128)S(1)}, u32[]{:S(2)}, u32[]{:S(2)}) %collective-permute-start.29) | collective-permute-done | bytes 1568 | tf_op jit(solution)/shard_map/ppermute | solution.py:39
  252.9 7.5 %collective-permute-done.30 = f32[4,3,32]{1,2,0:T(8,128)S(1)} collective-permute-done((f32[4,3,32]{1,2,0:T(8,128)S(1)}, f32[4,3,32]{1,2,0:T(8,128)S(1)}, u32[]{:S(2)}, u32[]{:S(2)}) %collective-permute-start.30) | collective-permute-done | bytes 1568 | tf_op jit(solution)/shard_map/ppermute | solution.py:39
  260.6 4.9 %collective-permute-start.23 = (f32[4,3,1080]{2,1,0:T(4,128)S(1)}, f32[4,3,1080]{2,1,0:T(4,128)S(1)}, u32[]{:S(2)}, u32[]{:S(2)}) collective-permute-start(f32[4,3,1080]{2,1,0:T(4,128)S(1)} %get-tuple-element.45), channel_id=1, source_target_pairs={{2,0},{4,2},{6,4},{8,6},{10,8},{12,10},{14,12},{0,14},{3,1},{5,3},... | collective-permute-start | bytes 155528 | tf_op jit(solution)/shard_map/ppermute | solution.py:17
  266.1 1.3 collective-permute-done.31
  268.0 0.6 gather_fusion.3
  269.0 0.5 collective-permute-start.32
  269.6 0.7 collective-permute-done.24
  270.4 0.4 maximum_maximum_fusion.2
  270.8 36.4 %fusion.54 = f32[4,32,1080]{2,1,0:T(8,128)S(1)} fusion(f32[4,38,1083]{2,1,0:T(8,128)S(1)} %get-tuple-element.31, f32[4,35,1080]{2,1,0:T(8,128)S(1)} %get-tuple-element.43, f32[4,38,1083]{2,1,0:T(8,128)S(1)} %get-tuple-element.30, f32[4,35,1080]{2,1,0:T(8,128)S(1)} %get-tuple-element.42, f32[3,32,1080]{2,1,0:T(8,128)S(1)} %broadcast_multiply_fusion.1, ...), kind=kLoop, calls=%fused_computation.141 | loop fusion | flops 13962240 | bytes 27924676 | tf_op jit(solution)/shard_map/mul | solution.py:98
  307.4 0.7 multiply_reduce_fusion
  308.1 33.8 %psum.37 = f32[]{:T(128)} all-reduce(f32[]{:T(128)} %get-tuple-element.19), channel_id=1, replica_groups=mesh['member'=2,'lon'=8,'lat'=2] {'lon','lat'}, use_global_device_ids=true, to_apply=%region_7.11 | all-reduce | flops 1 | bytes 8 | tf_op jit(solution)/shard_map/psum | solution.py:60
  342.9 6.9 %collective-permute-done.36 = f32[4,3,32]{1,2,0:T(8,128)S(1)} collective-permute-done((f32[4,3,32]{1,2,0:T(8,128)S(1)}, f32[4,3,32]{1,2,0:T(8,128)S(1)}, u32[]{:S(2)}, u32[]{:S(2)}) %collective-permute-start.36) | collective-permute-done | bytes 1568 | tf_op jit(solution)/shard_map/ppermute | solution.py:39
  349.9 7.5 %collective-permute-done.37 = f32[4,3,32]{1,2,0:T(8,128)S(1)} collective-permute-done((f32[4,3,32]{1,2,0:T(8,128)S(1)}, f32[4,3,32]{1,2,0:T(8,128)S(1)}, u32[]{:S(2)}, u32[]{:S(2)}) %collective-permute-start.37) | collective-permute-done | bytes 1568 | tf_op jit(solution)/shard_map/ppermute | solution.py:39
  357.4 7.0 %collective-permute-done.38 = f32[4,3,32]{1,2,0:T(8,128)S(1)} collective-permute-done((f32[4,3,32]{1,2,0:T(8,128)S(1)}, f32[4,3,32]{1,2,0:T(8,128)S(1)}, u32[]{:S(2)}, u32[]{:S(2)}) %collective-permute-start.38) | collective-permute-done | bytes 1568 | tf_op jit(solution)/shard_map/ppermute | solution.py:39
  364.3 7.0 %collective-permute-done.39 = f32[4,3,32]{1,2,0:T(8,128)S(1)} collective-permute-done((f32[4,3,32]{1,2,0:T(8,128)S(1)}, f32[4,3,32]{1,2,0:T(8,128)S(1)}, u32[]{:S(2)}, u32[]{:S(2)}) %collective-permute-start.39) | collective-permute-done | bytes 1568 | tf_op jit(solution)/shard_map/ppermute | solution.py:39
  371.3 7.0 %collective-permute-done.40 = f32[4,3,32]{1,2,0:T(8,128)S(1)} collective-permute-done((f32[4,3,32]{1,2,0:T(8,128)S(1)}, f32[4,3,32]{1,2,0:T(8,128)S(1)}, u32[]{:S(2)}, u32[]{:S(2)}) %collective-permute-start.40) | collective-permute-done | bytes 1568 | tf_op jit(solution)/shard_map/ppermute | solution.py:39
  378.3 4.8 %collective-permute-start.34 = (f32[4,3,1080]{2,1,0:T(4,128)S(1)}, f32[4,3,1080]{2,1,0:T(4,128)S(1)}, u32[]{:S(2)}, u32[]{:S(2)}) collective-permute-start(f32[4,3,1080]{2,1,0:T(4,128)S(1)} %get-tuple-element.41), channel_id=1, source_target_pairs={{2,0},{4,2},{6,4},{8,6},{10,8},{12,10},{14,12},{0,14},{3,1},{5,3},... | collective-permute-start | bytes 155528 | tf_op jit(solution)/shard_map/ppermute | solution.py:17
  383.1 2.1 collective-permute-done.41
  385.2 0.6 pad_maximum_fusion.28
  386.5 5.7 %collective-permute-done.42 = f32[4,3,32]{1,2,0:T(8,128)S(1)} collective-permute-done((f32[4,3,32]{1,2,0:T(8,128)S(1)}, f32[4,3,32]{1,2,0:T(8,128)S(1)}, u32[]{:S(2)}, u32[]{:S(2)}) %collective-permute-start.42) | collective-permute-done | bytes 1568 | tf_op jit(solution)/shard_map/ppermute | solution.py:39
  392.7 0.6 gather_fusion.4
  393.7 0.5 collective-permute-start.43
  394.3 0.7 collective-permute-done.35
  395.5 36.4 %fusion.3 = f32[4,32,1080]{2,1,0:T(8,128)S(1)} fusion(f32[4,38,1083]{2,1,0:T(8,128)S(1)} %get-tuple-element.27, f32[4,35,1080]{2,1,0:T(8,128)S(1)} %get-tuple-element.39, f32[4,38,1083]{2,1,0:T(8,128)S(1)} %get-tuple-element.26, f32[4,35,1080]{2,1,0:T(8,128)S(1)} %get-tuple-element.38, f32[3,32,1080]{2,1,0:T(8,128)S(1)} %broadcast_multiply_fusion, ...), kind=kLoop, calls=%fused_computation.42 | loop fusion | flops 13962240 | bytes 27924676 | tf_op jit(solution)/shard_map/mul | solution.py:98
  432.0 0.7 slice_bitcast_fusion
  432.6 0.8 slice.1702
  (158 shorter events, 9.5 us)
Async XLA Ops:
  0.6 42.7 %copy-start = (s32[256]{0:T(256)S(1)}, s32[256]{0:T(256)}, u32[]{:S(2)}) copy-start(s32[256]{0:T(256)} %param.18) | copy-start | bytes 3076
  0.6 8.9 %copy-start.5 = (f32[3,32,1080]{2,1,0:T(8,128)S(1)}, f32[3,32,1080]{2,1,0:T(8,128)}, u32[]{:S(2)}) copy-start(f32[3,32,1080]{2,1,0:T(8,128)} %param.13) | copy-start | bytes 1244164
  1.7 56.5 %collective-permute-start.14 = (f32[1,3,32]{1,2,0:T(8,128)S(1)}, f32[1,3,32]{1,2,0:T(8,128)S(1)}, u32[]{:S(2)}, u32[]{:S(2)}) collective-permute-start(f32[1,3,32]{1,2,0:T(8,128)S(1)} %slice_bitcast_fusion.1), channel_id=1, source_target_pairs={{0,2},{2,4},{4,6},{6,8},{8,10},{10,12},{12,14},{14,0},{1,3},{3,5},... | collective-permute-start | bytes 1160 | tf_op jit(solution)/shard_map/ppermute | solution.py:39
  4.7 108.1 %collective-permute-start.11 = (f32[1,3,1080]{2,1,0:T(4,128)S(1)}, f32[1,3,1080]{2,1,0:T(4,128)S(1)}, u32[]{:S(2)}, u32[]{:S(2)}) collective-permute-start(f32[1,3,1080]{2,1,0:T(4,128)S(1)} %get-tuple-element.63), channel_id=1, source_target_pairs={{0,2},{2,4},{4,6},{6,8},{8,10},{10,12},{12,14},{14,0},{1,3},{3,5},... | collective-permute-start | bytes 38888 | tf_op jit(solution)/shard_map/ppermute | solution.py:16
  6.3 3.3 copy-start.1
  6.3 3.3 copy-start.2
  6.3 3.3 copy-start.4
  6.3 106.6 %collective-permute-start.12 = (f32[1,3,1080]{2,1,0:T(4,128)S(1)}, f32[1,3,1080]{2,1,0:T(4,128)S(1)}, u32[]{:S(2)}, u32[]{:S(2)}) collective-permute-start(f32[1,3,1080]{2,1,0:T(4,128)S(1)} %get-tuple-element.64), channel_id=1, source_target_pairs={{2,0},{4,2},{6,4},{8,6},{10,8},{12,10},{14,12},{0,14},{3,1},{5,3},... | collective-permute-start | bytes 38888 | tf_op jit(solution)/shard_map/ppermute | solution.py:17
  9.6 1.0 copy-start.3
  43.2 7.4 %collective-permute-start.3 = (f32[4,3,32]{1,2,0:T(8,128)S(1)}, f32[4,3,32]{1,2,0:T(8,128)S(1)}, u32[]{:S(2)}, u32[]{:S(2)}) collective-permute-start(f32[4,3,32]{1,2,0:T(8,128)S(1)} %fusion.256), channel_id=1, source_target_pairs={{0,2},{2,4},{4,6},{6,8},{8,10},{10,12},{12,14},{14,0},{1,3},{3,5},... | collective-permute-start | bytes 4616 | tf_op jit(solution)/shard_map/ppermute | solution.py:39
  43.2 103.4 %collective-permute-start = (f32[4,3,1080]{2,1,0:T(4,128)S(1)}, f32[4,3,1080]{2,1,0:T(4,128)S(1)}, u32[]{:S(2)}, u32[]{:S(2)}) collective-permute-start(f32[4,3,1080]{2,1,0:T(4,128)S(1)} %get-tuple-element.48), channel_id=1, source_target_pairs={{0,2},{2,4},{4,6},{6,8},{8,10},{10,12},{12,14},{14,0},{1,3},{3,5},... | collective-permute-start | bytes 155528 | tf_op jit(solution)/shard_map/ppermute | solution.py:16
  43.4 0.8 copy-start.6
  50.5 7.0 %collective-permute-start.4 = (f32[4,3,32]{1,2,0:T(8,128)S(1)}, f32[4,3,32]{1,2,0:T(8,128)S(1)}, u32[]{:S(2)}, u32[]{:S(2)}) collective-permute-start(f32[4,3,32]{1,2,0:T(8,128)S(1)} %collective-permute-done.3), channel_id=1, source_target_pairs={{0,2},{2,4},{4,6},{6,8},{8,10},{10,12},{12,14},{14,0},{1,3},{3,5},... | collective-permute-start | bytes 4616 | tf_op jit(solution)/shard_map/ppermute | solution.py:39
  57.5 7.0 %collective-permute-start.5 = (f32[4,3,32]{1,2,0:T(8,128)S(1)}, f32[4,3,32]{1,2,0:T(8,128)S(1)}, u32[]{:S(2)}, u32[]{:S(2)}) collective-permute-start(f32[4,3,32]{1,2,0:T(8,128)S(1)} %collective-permute-done.4), channel_id=1, source_target_pairs={{0,2},{2,4},{4,6},{6,8},{8,10},{10,12},{12,14},{14,0},{1,3},{3,5},... | collective-permute-start | bytes 4616 | tf_op jit(solution)/shard_map/ppermute | solution.py:39
  58.2 6.5 %collective-permute-start.15 = (f32[1,3,32]{1,2,0:T(8,128)S(1)}, f32[1,3,32]{1,2,0:T(8,128)S(1)}, u32[]{:S(2)}, u32[]{:S(2)}) collective-permute-start(f32[1,3,32]{1,2,0:T(8,128)S(1)} %collective-permute-done.14), channel_id=1, source_target_pairs={{0,2},{2,4},{4,6},{6,8},{8,10},{10,12},{12,14},{14,0},{1,3},{3,5},... | collective-permute-start | bytes 1160 | tf_op jit(solution)/shard_map/ppermute | solution.py:39
  64.5 7.1 %collective-permute-start.6 = (f32[4,3,32]{1,2,0:T(8,128)S(1)}, f32[4,3,32]{1,2,0:T(8,128)S(1)}, u32[]{:S(2)}, u32[]{:S(2)}) collective-permute-start(f32[4,3,32]{1,2,0:T(8,128)S(1)} %collective-permute-done.5), channel_id=1, source_target_pairs={{0,2},{2,4},{4,6},{6,8},{8,10},{10,12},{12,14},{14,0},{1,3},{3,5},... | collective-permute-start | bytes 4616 | tf_op jit(solution)/shard_map/ppermute | solution.py:39
  64.7 6.9 %collective-permute-start.16 = (f32[1,3,32]{1,2,0:T(8,128)S(1)}, f32[1,3,32]{1,2,0:T(8,128)S(1)}, u32[]{:S(2)}, u32[]{:S(2)}) collective-permute-start(f32[1,3,32]{1,2,0:T(8,128)S(1)} %collective-permute-done.15), channel_id=1, source_target_pairs={{0,2},{2,4},{4,6},{6,8},{8,10},{10,12},{12,14},{14,0},{1,3},{3,5},... | collective-permute-start | bytes 1160 | tf_op jit(solution)/shard_map/ppermute | solution.py:39
  71.6 6.4 %collective-permute-start.17 = (f32[1,3,32]{1,2,0:T(8,128)S(1)}, f32[1,3,32]{1,2,0:T(8,128)S(1)}, u32[]{:S(2)}, u32[]{:S(2)}) collective-permute-start(f32[1,3,32]{1,2,0:T(8,128)S(1)} %collective-permute-done.16), channel_id=1, source_target_pairs={{0,2},{2,4},{4,6},{6,8},{8,10},{10,12},{12,14},{14,0},{1,3},{3,5},... | collective-permute-start | bytes 1160 | tf_op jit(solution)/shard_map/ppermute | solution.py:39
  71.6 26.1 %collective-permute-start.7 = (f32[4,3,32]{1,2,0:T(8,128)S(1)}, f32[4,3,32]{1,2,0:T(8,128)S(1)}, u32[]{:S(2)}, u32[]{:S(2)}) collective-permute-start(f32[4,3,32]{1,2,0:T(8,128)S(1)} %collective-permute-done.6), channel_id=1, source_target_pairs={{0,2},{2,4},{4,6},{6,8},{8,10},{10,12},{12,14},{14,0},{1,3},{3,5},... | collective-permute-start | bytes 4616 | tf_op jit(solution)/shard_map/ppermute | solution.py:39
  78.0 6.4 %collective-permute-start.18 = (f32[1,3,32]{1,2,0:T(8,128)S(1)}, f32[1,3,32]{1,2,0:T(8,128)S(1)}, u32[]{:S(2)}, u32[]{:S(2)}) collective-permute-start(f32[1,3,32]{1,2,0:T(8,128)S(1)} %collective-permute-done.17), channel_id=1, source_target_pairs={{0,2},{2,4},{4,6},{6,8},{8,10},{10,12},{12,14},{14,0},{1,3},{3,5},... | collective-permute-start | bytes 1160 | tf_op jit(solution)/shard_map/ppermute | solution.py:39
  84.5 6.5 %collective-permute-start.19 = (f32[1,3,32]{1,2,0:T(8,128)S(1)}, f32[1,3,32]{1,2,0:T(8,128)S(1)}, u32[]{:S(2)}, u32[]{:S(2)}) collective-permute-start(f32[1,3,32]{1,2,0:T(8,128)S(1)} %collective-permute-done.18), channel_id=1, source_target_pairs={{0,2},{2,4},{4,6},{6,8},{8,10},{10,12},{12,14},{14,0},{1,3},{3,5},... | collective-permute-start | bytes 1160 | tf_op jit(solution)/shard_map/ppermute | solution.py:39
  91.0 6.4 %collective-permute-start.20 = (f32[1,3,32]{1,2,0:T(8,128)S(1)}, f32[1,3,32]{1,2,0:T(8,128)S(1)}, u32[]{:S(2)}, u32[]{:S(2)}) collective-permute-start(f32[1,3,32]{1,2,0:T(8,128)S(1)} %collective-permute-done.19), channel_id=1, source_target_pairs={{0,2},{2,4},{4,6},{6,8},{8,10},{10,12},{12,14},{14,0},{1,3},{3,5},... | collective-permute-start | bytes 1160 | tf_op jit(solution)/shard_map/ppermute | solution.py:39
  97.4 49.2 %collective-permute-start.1 = (f32[4,3,1080]{2,1,0:T(4,128)S(1)}, f32[4,3,1080]{2,1,0:T(4,128)S(1)}, u32[]{:S(2)}, u32[]{:S(2)}) collective-permute-start(f32[4,3,1080]{2,1,0:T(4,128)S(1)} %get-tuple-element.49), channel_id=1, source_target_pairs={{2,0},{4,2},{6,4},{8,6},{10,8},{12,10},{14,12},{0,14},{3,1},{5,3},... | collective-permute-start | bytes 155528 | tf_op jit(solution)/shard_map/ppermute | solution.py:17
  97.7 7.0 %collective-permute-start.8 = (f32[4,3,32]{1,2,0:T(8,128)S(1)}, f32[4,3,32]{1,2,0:T(8,128)S(1)}, u32[]{:S(2)}, u32[]{:S(2)}) collective-permute-start(f32[4,3,32]{1,2,0:T(8,128)S(1)} %collective-permute-done.7), channel_id=1, source_target_pairs={{0,2},{2,4},{4,6},{6,8},{8,10},{10,12},{12,14},{14,0},{1,3},{3,5},... | collective-permute-start | bytes 4616 | tf_op jit(solution)/shard_map/ppermute | solution.py:39
  104.7 7.0 %collective-permute-start.9 = (f32[4,3,32]{1,2,0:T(8,128)S(1)}, f32[4,3,32]{1,2,0:T(8,128)S(1)}, u32[]{:S(2)}, u32[]{:S(2)}) collective-permute-start(f32[4,3,32]{1,2,0:T(8,128)S(1)} %collective-permute-done.8), channel_id=1, source_target_pairs={{0,2},{2,4},{4,6},{6,8},{8,10},{10,12},{12,14},{14,0},{1,3},{3,5},... | collective-permute-start | bytes 4616 | tf_op jit(solution)/shard_map/ppermute | solution.py:39
  112.9 1.2 collective-permute-start.13
  113.1 1.4 collective-permute-start.21
  146.8 1.3 collective-permute-start.2
  147.2 1.3 collective-permute-start.10
  217.4 7.0 %collective-permute-start.25 = (f32[4,3,32]{1,2,0:T(8,128)S(1)}, f32[4,3,32]{1,2,0:T(8,128)S(1)}, u32[]{:S(2)}, u32[]{:S(2)}) collective-permute-start(f32[4,3,32]{1,2,0:T(8,128)S(1)} %fusion.254), channel_id=1, source_target_pairs={{0,2},{2,4},{4,6},{6,8},{8,10},{10,12},{12,14},{14,0},{1,3},{3,5},... | collective-permute-start | bytes 4616 | tf_op jit(solution)/shard_map/ppermute | solution.py:39
  224.4 7.0 %collective-permute-start.26 = (f32[4,3,32]{1,2,0:T(8,128)S(1)}, f32[4,3,32]{1,2,0:T(8,128)S(1)}, u32[]{:S(2)}, u32[]{:S(2)}) collective-permute-start(f32[4,3,32]{1,2,0:T(8,128)S(1)} %collective-permute-done.25), channel_id=1, source_target_pairs={{0,2},{2,4},{4,6},{6,8},{8,10},{10,12},{12,14},{14,0},{1,3},{3,5},... | collective-permute-start | bytes 4616 | tf_op jit(solution)/shard_map/ppermute | solution.py:39
  231.3 7.0 %collective-permute-start.27 = (f32[4,3,32]{1,2,0:T(8,128)S(1)}, f32[4,3,32]{1,2,0:T(8,128)S(1)}, u32[]{:S(2)}, u32[]{:S(2)}) collective-permute-start(f32[4,3,32]{1,2,0:T(8,128)S(1)} %collective-permute-done.26), channel_id=1, source_target_pairs={{0,2},{2,4},{4,6},{6,8},{8,10},{10,12},{12,14},{14,0},{1,3},{3,5},... | collective-permute-start | bytes 4616 | tf_op jit(solution)/shard_map/ppermute | solution.py:39
  238.3 7.0 %collective-permute-start.28 = (f32[4,3,32]{1,2,0:T(8,128)S(1)}, f32[4,3,32]{1,2,0:T(8,128)S(1)}, u32[]{:S(2)}, u32[]{:S(2)}) collective-permute-start(f32[4,3,32]{1,2,0:T(8,128)S(1)} %collective-permute-done.27), channel_id=1, source_target_pairs={{0,2},{2,4},{4,6},{6,8},{8,10},{10,12},{12,14},{14,0},{1,3},{3,5},... | collective-permute-start | bytes 4616 | tf_op jit(solution)/shard_map/ppermute | solution.py:39
  245.3 7.6 %collective-permute-start.29 = (f32[4,3,32]{1,2,0:T(8,128)S(1)}, f32[4,3,32]{1,2,0:T(8,128)S(1)}, u32[]{:S(2)}, u32[]{:S(2)}) collective-permute-start(f32[4,3,32]{1,2,0:T(8,128)S(1)} %collective-permute-done.28), channel_id=1, source_target_pairs={{0,2},{2,4},{4,6},{6,8},{8,10},{10,12},{12,14},{14,0},{1,3},{3,5},... | collective-permute-start | bytes 4616 | tf_op jit(solution)/shard_map/ppermute | solution.py:39
  252.9 7.6 %collective-permute-start.30 = (f32[4,3,32]{1,2,0:T(8,128)S(1)}, f32[4,3,32]{1,2,0:T(8,128)S(1)}, u32[]{:S(2)}, u32[]{:S(2)}) collective-permute-start(f32[4,3,32]{1,2,0:T(8,128)S(1)} %collective-permute-done.29), channel_id=1, source_target_pairs={{0,2},{2,4},{4,6},{6,8},{8,10},{10,12},{12,14},{14,0},{1,3},{3,5},... | collective-permute-start | bytes 4616 | tf_op jit(solution)/shard_map/ppermute | solution.py:39
  260.4 7.0 %collective-permute-start.31 = (f32[4,3,32]{1,2,0:T(8,128)S(1)}, f32[4,3,32]{1,2,0:T(8,128)S(1)}, u32[]{:S(2)}, u32[]{:S(2)}) collective-permute-start(f32[4,3,32]{1,2,0:T(8,128)S(1)} %collective-permute-done.30), channel_id=1, source_target_pairs={{0,2},{2,4},{4,6},{6,8},{8,10},{10,12},{12,14},{14,0},{1,3},{3,5},... | collective-permute-start | bytes 4616 | tf_op jit(solution)/shard_map/ppermute | solution.py:39
  260.6 8.2 %collective-permute-start.22 = (f32[4,3,1080]{2,1,0:T(4,128)S(1)}, f32[4,3,1080]{2,1,0:T(4,128)S(1)}, u32[]{:S(2)}, u32[]{:S(2)}) collective-permute-start(f32[4,3,1080]{2,1,0:T(4,128)S(1)} %get-tuple-element.44), channel_id=1, source_target_pairs={{0,2},{2,4},{4,6},{6,8},{8,10},{10,12},{12,14},{14,0},{1,3},{3,5},... | collective-permute-start | bytes 155528 | tf_op jit(solution)/shard_map/ppermute | solution.py:16
  260.6 8.2 %collective-permute-start.23 = (f32[4,3,1080]{2,1,0:T(4,128)S(1)}, f32[4,3,1080]{2,1,0:T(4,128)S(1)}, u32[]{:S(2)}, u32[]{:S(2)}) collective-permute-start(f32[4,3,1080]{2,1,0:T(4,128)S(1)} %get-tuple-element.45), channel_id=1, source_target_pairs={{2,0},{4,2},{6,4},{8,6},{10,8},{12,10},{14,12},{0,14},{3,1},{5,3},... | collective-permute-start | bytes 155528 | tf_op jit(solution)/shard_map/ppermute | solution.py:17
  268.9 1.3 collective-permute-start.24
  269.0 1.4 collective-permute-start.32
  342.9 7.0 %collective-permute-start.36 = (f32[4,3,32]{1,2,0:T(8,128)S(1)}, f32[4,3,32]{1,2,0:T(8,128)S(1)}, u32[]{:S(2)}, u32[]{:S(2)}) collective-permute-start(f32[4,3,32]{1,2,0:T(8,128)S(1)} %fusion.252), channel_id=1, source_target_pairs={{0,2},{2,4},{4,6},{6,8},{8,10},{10,12},{12,14},{14,0},{1,3},{3,5},... | collective-permute-start | bytes 4616 | tf_op jit(solution)/shard_map/ppermute | solution.py:39
  349.9 7.5 %collective-permute-start.37 = (f32[4,3,32]{1,2,0:T(8,128)S(1)}, f32[4,3,32]{1,2,0:T(8,128)S(1)}, u32[]{:S(2)}, u32[]{:S(2)}) collective-permute-start(f32[4,3,32]{1,2,0:T(8,128)S(1)} %collective-permute-done.36), channel_id=1, source_target_pairs={{0,2},{2,4},{4,6},{6,8},{8,10},{10,12},{12,14},{14,0},{1,3},{3,5},... | collective-permute-start | bytes 4616 | tf_op jit(solution)/shard_map/ppermute | solution.py:39
  357.4 7.0 %collective-permute-start.38 = (f32[4,3,32]{1,2,0:T(8,128)S(1)}, f32[4,3,32]{1,2,0:T(8,128)S(1)}, u32[]{:S(2)}, u32[]{:S(2)}) collective-permute-start(f32[4,3,32]{1,2,0:T(8,128)S(1)} %collective-permute-done.37), channel_id=1, source_target_pairs={{0,2},{2,4},{4,6},{6,8},{8,10},{10,12},{12,14},{14,0},{1,3},{3,5},... | collective-permute-start | bytes 4616 | tf_op jit(solution)/shard_map/ppermute | solution.py:39
  364.3 7.0 %collective-permute-start.39 = (f32[4,3,32]{1,2,0:T(8,128)S(1)}, f32[4,3,32]{1,2,0:T(8,128)S(1)}, u32[]{:S(2)}, u32[]{:S(2)}) collective-permute-start(f32[4,3,32]{1,2,0:T(8,128)S(1)} %collective-permute-done.38), channel_id=1, source_target_pairs={{0,2},{2,4},{4,6},{6,8},{8,10},{10,12},{12,14},{14,0},{1,3},{3,5},... | collective-permute-start | bytes 4616 | tf_op jit(solution)/shard_map/ppermute | solution.py:39
  371.3 7.0 %collective-permute-start.40 = (f32[4,3,32]{1,2,0:T(8,128)S(1)}, f32[4,3,32]{1,2,0:T(8,128)S(1)}, u32[]{:S(2)}, u32[]{:S(2)}) collective-permute-start(f32[4,3,32]{1,2,0:T(8,128)S(1)} %collective-permute-done.39), channel_id=1, source_target_pairs={{0,2},{2,4},{4,6},{6,8},{8,10},{10,12},{12,14},{14,0},{1,3},{3,5},... | collective-permute-start | bytes 4616 | tf_op jit(solution)/shard_map/ppermute | solution.py:39
  378.2 7.0 %collective-permute-start.41 = (f32[4,3,32]{1,2,0:T(8,128)S(1)}, f32[4,3,32]{1,2,0:T(8,128)S(1)}, u32[]{:S(2)}, u32[]{:S(2)}) collective-permute-start(f32[4,3,32]{1,2,0:T(8,128)S(1)} %collective-permute-done.40), channel_id=1, source_target_pairs={{0,2},{2,4},{4,6},{6,8},{8,10},{10,12},{12,14},{14,0},{1,3},{3,5},... | collective-permute-start | bytes 4616 | tf_op jit(solution)/shard_map/ppermute | solution.py:39
  378.3 15.2 %collective-permute-start.33 = (f32[4,3,1080]{2,1,0:T(4,128)S(1)}, f32[4,3,1080]{2,1,0:T(4,128)S(1)}, u32[]{:S(2)}, u32[]{:S(2)}) collective-permute-start(f32[4,3,1080]{2,1,0:T(4,128)S(1)} %get-tuple-element.40), channel_id=1, source_target_pairs={{0,2},{2,4},{4,6},{6,8},{8,10},{10,12},{12,14},{14,0},{1,3},{3,5},... | collective-permute-start | bytes 155528 | tf_op jit(solution)/shard_map/ppermute | solution.py:16
  378.3 15.2 %collective-permute-start.34 = (f32[4,3,1080]{2,1,0:T(4,128)S(1)}, f32[4,3,1080]{2,1,0:T(4,128)S(1)}, u32[]{:S(2)}, u32[]{:S(2)}) collective-permute-start(f32[4,3,1080]{2,1,0:T(4,128)S(1)} %get-tuple-element.41), channel_id=1, source_target_pairs={{2,0},{4,2},{6,4},{8,6},{10,8},{12,10},{14,12},{0,14},{3,1},{5,3},... | collective-permute-start | bytes 155528 | tf_op jit(solution)/shard_map/ppermute | solution.py:17
  385.2 7.0 %collective-permute-start.42 = (f32[4,3,32]{1,2,0:T(8,128)S(1)}, f32[4,3,32]{1,2,0:T(8,128)S(1)}, u32[]{:S(2)}, u32[]{:S(2)}) collective-permute-start(f32[4,3,32]{1,2,0:T(8,128)S(1)} %collective-permute-done.41), channel_id=1, source_target_pairs={{0,2},{2,4},{4,6},{6,8},{8,10},{10,12},{12,14},{14,0},{1,3},{3,5},... | collective-permute-start | bytes 4616 | tf_op jit(solution)/shard_map/ppermute | solution.py:39
  393.6 1.3 collective-permute-start.35
  393.7 1.4 collective-permute-start.43
